TPU v7x, 32 devices: a whole 2x2x4 slice. The times are simulated.
32 devices in a mesh: feat: 8 (over z, y), samp: 4 (over x, core).
Axes of the slice: x: 2, y: 2, z: 4, core: 2. Of those that a mesh axis runs over, the one named last changes fastest.
Arguments:
- design: bfloat16 [14336, 8192], P('samp', 'feat'), may hold values from -0.0625 to 0.0625
- targets: bfloat16 [14336, 128], P('samp'), may hold values from -26 to 26
- warm_start: float32 [8192, 128], P('feat'), may hold values from -0.6 to 0.6
- active_mask: int32 [2, 8192], P(None, 'feat'), may hold values 0 or 1
- penalty_index: int32 [1], replicated, may hold values from 0 to 7
Outputs:
- coefficients: float32 [8192, 128], P('feat')
- correlations: float32 [3, 8192], P(None, 'feat')
- relative_gaps: float32 [3], replicated
- pruned_counts: float32 [2], replicated
All inputs are finite; a program needn't handle non-finite values. No bound on the sum of `active_mask` on one device may be relied on, other than what follows from the above.
Results may differ from a plain program's by a relative error of at most 0.0024.
The roundings to bfloat16 on the way count: a program that leaves them out, or rounds other values in their place, can miss the bound.
Values may be sent and summed in bfloat16 or wider, within the bound.
A program may use at most 64 MiB of HBM per device.

v0:
```python
import jax
import jax.numpy as jnp
from jax import lax
from jax.sharding import PartitionSpec as P

ITERS = 2


def group_norms(matrix):
    return jnp.sqrt(jnp.sum(matrix * matrix, axis=1))


def transpose_product(design, right_side):
    return lax.dot_general(
        design, right_side, (((0,), (0,)), ((), ())), preferred_element_type=jnp.float32
    )


def local(design, targets, warm_start, active_mask, penalty_index):
    row_count, col_count = design.shape
    feat_size = lax.axis_size("feat")
    feat_slot = lax.axis_index("feat")
    block_rows = row_count // feat_size
    samp_first = (lax.axis_index("samp") == 0).astype(jnp.float32)
    corr_local = transpose_product(design, targets)
    squares_local = jnp.sum(jnp.square(design.astype(jnp.float32)), axis=0)
    corr_y, column_squares = lax.psum((corr_local, squares_local), "samp")
    penalty_max = lax.pmax(jnp.max(group_norms(corr_y)), "feat")
    penalty = penalty_max / (8.0 + 4.0 * penalty_index[0].astype(jnp.float32))
    step_sizes = 0.5 / (1.0 + column_squares)
    current = warm_start
    correlations = []
    relative_gaps = []
    pruned_counts = []
    own_targets = lax.dynamic_slice_in_dim(targets, feat_slot * block_rows, block_rows, 0)
    for iteration in range(ITERS + 1):
        current_half = current.astype(jnp.bfloat16)
        fitted_part = jnp.dot(design, current_half, preferred_element_type=jnp.float32)
        fitted = lax.psum(fitted_part, "feat")
        residual_all = (targets.astype(jnp.float32) - fitted).astype(jnp.bfloat16)
        residual = lax.dynamic_slice_in_dim(residual_all, feat_slot * block_rows, block_rows, 0)
        grad_local = transpose_product(design, residual_all)
        resid_float = residual.astype(jnp.float32)
        rr_local = jnp.sum(resid_float * resid_float)
        ry_local = jnp.sum(resid_float * own_targets.astype(jnp.float32))
        bn_local = samp_first * jnp.sum(group_norms(current))
        if iteration < ITERS:
            keep = active_mask[iteration].astype(jnp.float32)
            pruned_local = samp_first * jnp.sum(1.0 - keep)
        else:
            pruned_local = jnp.zeros((), jnp.float32)
        gradient = lax.psum(grad_local, "samp")
        grad_norms = group_norms(gradient)
        local_max = jnp.max(grad_norms)
        grad_top = lax.pmax(local_max, "feat")
        rr_sum, ry_sum, bn_sum, pruned_sum = lax.psum(
            (rr_local, ry_local, bn_local, pruned_local), ("feat", "samp")
        )
        scale = jnp.maximum(penalty, grad_top)
        correlations.append(grad_norms / scale)
        primal = 0.5 * rr_sum + penalty * bn_sum
        ratio = penalty / scale
        dual = ratio * ry_sum - 0.5 * ratio * ratio * rr_sum
        relative_gaps.append((primal - dual) / (primal + 1.0))
        if iteration < ITERS:
            pruned_counts.append(pruned_sum)
            moved = current + step_sizes[:, None] * gradient
            moved_norms = group_norms(moved)
            cutoff = step_sizes * penalty
            factor = jnp.maximum(moved_norms - cutoff, 0.0) / jnp.maximum(moved_norms, cutoff)
            current = (keep * factor)[:, None] * moved
    return (current, jnp.stack(correlations), jnp.stack(relative_gaps), jnp.stack(pruned_counts))


def solution(mesh):
    placed = (P("samp", "feat"), P("samp", None), P("feat", None), P(None, "feat"), P())
    return jax.shard_map(
        local,
        mesh=mesh,
        in_specs=placed,
        out_specs=(P("feat", None), P(None, "feat"), P(), P()),
        check_vma=False,
    )
```

profile of v0, /device:TPU:0, one launch (start us, length us, event | category | flops | bytes accessed | tf_op | source)
XLA Modules:
  0.0 527.3 jit_solution(8647449387170644454)
XLA Ops:
  7.2 6.5 %fusion.5 = f32[3584,128]{1,0:T(8,128)} fusion(bf16[3584,1024]{1,0:T(8,128)(2,1)} %param.5, f32[1024,128]{1,0:T(8,128)} %param.7), kind=kOutput, calls=%fused_computation.33 | convolution fusion | flops 939655168 | bytes 9699328 | tf_op jit(solution)/shard_map/dot_general | solution.py:38
  13.8 6.0 %fusion.13 = f32[1024,128]{1,0:T(8,128)} fusion(bf16[3584,1024]{1,0:T(8,128)(2,1)} %param.5, bf16[3584,128]{1,0:T(8,128)(2,1)S(1)} %copy-done), kind=kOutput, calls=%fused_computation.61 | convolution fusion | flops 939524096 | bytes 8781824 | tf_op jit(solution)/shard_map/dot_general | solution.py:14
  19.8 92.7 %all-reduce.10.cloned.1.call-done = f32[3584,128]{1,0:T(8,128)} async-done(((f32[3584,128]{1,0:T(8,128)}), f32[3584,128]{1,0:T(8,128)}) %all-reduce.10.cloned.1.call-update) | async-done | bytes 1835024 | tf_op jit(solution)/shard_map/psum | solution.py:39
  112.5 1.7 fusion
  114.1 5.0 convolution_bitcast_fusion.4
  119.3 4.6 multiply_reduce_fusion
  125.5 7.1 %psum.133 = f32[1024]{0:T(1024)S(1)} all-reduce(f32[1024]{0:T(1024)S(1)} %multiply_reduce_fusion), channel_id=1, replica_groups=mesh['feat'=8,'samp'=4] {'samp'}, use_global_device_ids=true, to_apply=%region_1.0 | all-reduce | flops 1024 | bytes 8192 | tf_op jit(solution)/shard_map/psum | solution.py:27
  132.7 22.5 %all-reduce.20.cloned.1.call-done = (f32[1024,128]{0,1:T(8,128)}, f32[1024,128]{1,0:T(8,128)}) async-done(((f32[1024,128]{0,1:T(8,128)}, f32[1024,128]{1,0:T(8,128)}), (f32[1024,128]{0,1:T(8,128)}, f32[1024,128]{1,0:T(8,128)})) %all-reduce.20.cloned.1.call-update) | async-done | bytes 1048592 | tf_op jit(solution)/shard_map/psum | solution.py:52
  155.2 1.2 multiply_reduce_fusion.8
  157.1 22.0 %pmax.28 = f32[]{:T(128)} all-reduce(f32[]{:T(128)} %sqrt_reduce_fusion.3), channel_id=1, replica_groups=mesh['feat'=8,'samp'=4] {'feat'}, use_global_device_ids=true, to_apply=%region_8.0 | all-reduce | flops 1 | bytes 8 | tf_op jit(solution)/shard_map/pmax | solution.py:28
  179.7 1.3 multiply_reduce_fusion.9
  181.7 6.4 %convolution_bitcast_fusion.1 = f32[3584,128]{1,0:T(8,128)} fusion(bf16[3584,1024]{1,0:T(8,128)(2,1)} %param.5, f32[1024,128]{0,1:T(8,128)S(1)} %get-tuple-element.36, f32[1024]{0:T(1024)S(1)} %get-tuple-element.41), kind=kOutput, calls=%fused_computation.2 | convolution fusion | flops 939786240 | bytes 9703424 | tf_op jit(solution)/shard_map/dot_general | solution.py:38
  188.1 92.7 %all-reduce.12.cloned.1.call-done = f32[3584,128]{1,0:T(8,128)} async-done(((f32[3584,128]{1,0:T(8,128)}), f32[3584,128]{1,0:T(8,128)}) %all-reduce.12.cloned.1.call-update) | async-done | bytes 1835024 | tf_op jit(solution)/shard_map/psum | solution.py:39
  280.9 1.7 fusion.1
  282.6 5.0 convolution_bitcast_fusion.3
  287.8 32.8 %all-reduce.14.cloned.1.call-done = f32[1024,128]{0,1:T(8,128)} async-done(((f32[1024,128]{0,1:T(8,128)}), f32[1024,128]{0,1:T(8,128)}) %all-reduce.14.cloned.1.call-update) | async-done | bytes 524304 | tf_op jit(solution)/shard_map/psum | solution.py:52
  324.5 6.4 %convolution_bitcast_fusion = f32[3584,128]{1,0:T(8,128)} fusion(bf16[3584,1024]{1,0:T(8,128)(2,1)} %param.5, f32[1024,128]{0,1:T(8,128)S(1)} %get-tuple-element.34), kind=kOutput, calls=%fused_computation.1 | convolution fusion | flops 939655168 | bytes 9699328 | tf_op jit(solution)/shard_map/dot_general | solution.py:38
  334.3 92.8 %all-reduce.16.cloned.1.call-done = f32[3584,128]{1,0:T(8,128)} async-done(((f32[3584,128]{1,0:T(8,128)}), f32[3584,128]{1,0:T(8,128)}) %all-reduce.16.cloned.1.call-update) | async-done | bytes 1835024 | tf_op jit(solution)/shard_map/psum | solution.py:39
  427.1 1.7 fusion.2
  429.7 5.1 convolution_bitcast_fusion.2
  439.0 1.7 fusion.10
  440.7 41.8 %all-reduce = (f32[]{:T(128)}, f32[]{:T(128)}, f32[]{:T(128)}, f32[]{:T(128)}, f32[]{:T(128)}, /*index=5*/f32[]{:T(128)}, f32[]{:T(128)}, f32[]{:T(128)}, f32[]{:T(128)}, f32[1]{0:T(128)}, /*index=10*/f32[1]{0:T(128)}) all-reduce(f32[]{:T(128)} %get-tuple-element.12, ...), channel_id=1, replica_groups=mesh['feat'=8,'samp'=4] {'feat','samp'}, use_global_device_ids=true, to_apply=%region_38.0 | all-reduce | flops 11 | bytes 88 | tf_op jit(solution)/shard_map/psum | solution.py:56
  486.2 1.9 pad_maximum_fusion.2
  489.9 21.7 %all-reduce.1 = (f32[]{:T(128)}, f32[]{:T(128)}, f32[]{:T(128)}) all-reduce(f32[]{:T(128)} %sqrt_reduce_fusion.4, f32[]{:T(128)} %sqrt_reduce_fusion.5, f32[]{:T(128)} %sqrt_reduce_fusion.6), channel_id=1, replica_groups=mesh['feat'=8,'samp'=4] {'feat'}, use_global_device_ids=true, to_apply=%region_22.0 | all-reduce | flops 3 | bytes 24 | tf_op jit(solution)/shard_map/pmax | solution.py:55
  (49 shorter events, 14.8 us)
Async XLA Ops:
  7.2 6.6 %copy-start = (bf16[3584,128]{1,0:T(8,128)(2,1)S(1)}, bf16[3584,128]{1,0:T(8,128)(2,1)}, u32[]{:S(2)}) copy-start(bf16[3584,128]{1,0:T(8,128)(2,1)} %param.6) | copy-start | bytes 2752516
  7.2 105.3 %all-reduce.10.cloned.1.call-start = ((), (), s32[]{:S(2)}) async-start(), calls=%async_computation | async-start | bytes 3670016 | tf_op jit(solution)/shard_map/psum | solution.py:39
  13.7 141.5 %all-reduce.20.cloned.1.call-start = ((), (), s32[]{:S(2)}) async-start(), calls=%async_computation.5 | async-start | bytes 2097152 | tf_op jit(solution)/shard_map/psum | solution.py:52
  119.2 4.7 copy-start.4
  119.2 13.5 %copy-start.6 = (s32[2,1024]{1,0:T(2,128)S(1)}, s32[2,1024]{1,0:T(2,128)}, u32[]{:S(2)}) copy-start(s32[2,1024]{1,0:T(2,128)} %param.8) | copy-start | bytes 24580
  119.2 161.7 %all-reduce.12.cloned.1.call-start = ((), (), s32[]{:S(2)}) async-start(), calls=%async_computation.1 | async-start | bytes 3670016 | tf_op jit(solution)/shard_map/psum | solution.py:39
  188.1 132.6 %all-reduce.14.cloned.1.call-start = ((), (), s32[]{:S(2)}) async-start(), calls=%async_computation.2 | async-start | bytes 1048576 | tf_op jit(solution)/shard_map/psum | solution.py:52
  287.6 139.5 %all-reduce.16.cloned.1.call-start = ((), (), s32[]{:S(2)}) async-start(), calls=%async_computation.3 | async-start | bytes 3670016 | tf_op jit(solution)/shard_map/psum | solution.py:39
  323.7 0.8 copy-start.2
  323.8 7.3 %copy-start.5 = (f32[1024,128]{1,0:T(8,128)S(1)}, f32[1024,128]{1,0:T(8,128)}, u32[]{:S(2)}) copy-start(f32[1024,128]{1,0:T(8,128)} %param.7) | copy-start | bytes 1572868
  331.0 157.1 %all-reduce.18.cloned.1.call-start = ((), (), s32[]{:S(2)}) async-start(), calls=%async_computation.4 | async-start | bytes 1048576 | tf_op jit(solution)/shard_map/psum | solution.py:52
  428.7 0.9 copy-start.1
  429.7 5.8 %copy-start.3 = (f32[1024,128]{0,1:T(8,128)S(1)}, f32[1024,128]{0,1:T(8,128)}, u32[]{:S(2)}) copy-start(f32[1024,128]{0,1:T(8,128)} %copy-done.2) | copy-start | bytes 1572868
Sparse Core Ops, SparseCore 0:
  13.9 98.5 all-reduce.9
  119.3 35.8 all-reduce.19
  188.2 92.6 all-reduce.11
  287.7 32.9 all-reduce.13
  331.1 95.9 all-reduce.15
  434.9 33.1 all-reduce.17
where the time goes:
time: 528 us; the launch traced here: 527 us
  waiting for transfers between devices  334 us (63%)
  blocking collectives  92.5 us (18%)
  matrix products  40.5 us (8%)
  between operations  30.1 us (6%)
  other arithmetic  26.4 us (5%)
    psum x3, waiting for transfers between devices, local(): fitted = lax.psum(fitted_part, 'feat')  278 us
    psum x3, waiting for transfers between devices, local(): gradient = lax.psum(grad_local, 'samp')  55.4 us
    psum x1, blocking collectives, local(): lax.psum((rr_local, ry_local, bn_local, pruned_local), ('feat', 'samp'))  41.8 us
    pmax x1, blocking collectives, local(): penalty_max = lax.pmax(jnp.max(group_norms(corr_y)), 'feat')  22 us
    pmax x1, blocking collectives, local(): grad_top = lax.pmax(local_max, 'feat')  21.7 us
    dot_general x4, matrix products, transpose_product(): lax.dot_general(design, right_side, (((0,), (0,)), ((), ())), preferred_e...  21.2 us
    dot_general x3, matrix products, local(): jnp.dot(design, current_half, preferred_element_type=jnp.float32)  19.3 us
  transfers between devices with their start and end apart: 6, of which 5 were waited for; matrix products, arithmetic and copies ran while one was open for 4% of the time, Pallas kernels for 0%

commit v1 on v0

--- a/solution.py
+++ b/solution.py
@@ -36,7 +36,7 @@
     for iteration in range(ITERS + 1):
         current_half = current.astype(jnp.bfloat16)
         fitted_part = jnp.dot(design, current_half, preferred_element_type=jnp.float32)
-        fitted = lax.psum(fitted_part, "feat")
+        fitted = jnp.sum(lax.all_gather(fitted_part, axis_name="feat"), 0)
         residual_all = (targets.astype(jnp.float32) - fitted).astype(jnp.bfloat16)
         residual = lax.dynamic_slice_in_dim(residual_all, feat_slot * block_rows, block_rows, 0)
         grad_local = transpose_product(design, residual_all)

time: 528 us -> 927 us (1.76)
  waiting for transfers between devices: 334 us -> 650 us
  local copies, waits for them, and re-layouts: 3.71 us -> 52 us
  other arithmetic: 26.4 us -> 53.5 us
    all_gather x0 -> x3, waiting for transfers between devices: none -> 595 us  [local(): fitted = jnp.sum(lax.all_gather(fitted_part, axis_name='feat'), 0)]
    psum x3 -> x0, waiting for transfers between devices: 278 us -> none  [local(): fitted = lax.psum(fitted_part, 'feat')]
    unnamed x16 -> x18, local copies, waits for them, and re-layouts: 3.71 us -> 46.5 us
    reduce_sum x0 -> x3, other arithmetic: none -> 27.3 us  [local(): fitted = jnp.sum(lax.all_gather(fitted_part, axis_name='feat'), 0)]
  transfers between devices with their start and end apart: 6 -> 6, of which waited for: 5 -> 5; matrix products, arithmetic and copies ran while one was open for 4% -> 2% of each run, Pallas kernels for 0% -> 0%
where the time goes in v1:
time: 927 us; the launch traced here: 918 us
  waiting for transfers between devices  650 us (70%)
  blocking collectives  90.5 us (10%)
  other arithmetic  53.5 us (6%)
  local copies, waits for them, and re-layouts  52 us (6%)
  matrix products  41.4 us (4%)
  between operations  30.4 us (3%)
    all_gather x3, waiting for transfers between devices, local(): fitted = jnp.sum(lax.all_gather(fitted_part, axis_name='feat'), 0)  595 us
    psum x3, waiting for transfers between devices, local(): gradient = lax.psum(grad_local, 'samp')  54.4 us
    unnamed x18, local copies, waits for them, and re-layouts  46.5 us
    psum x1, blocking collectives, local(): lax.psum((rr_local, ry_local, bn_local, pruned_local), ('feat', 'samp'))  40 us
    reduce_sum x3, other arithmetic, local(): fitted = jnp.sum(lax.all_gather(fitted_part, axis_name='feat'), 0)  27.3 us
    pmax x1, blocking collectives, local(): grad_top = lax.pmax(local_max, 'feat')  22.1 us
    pmax x1, blocking collectives, local(): penalty_max = lax.pmax(jnp.max(group_norms(corr_y)), 'feat')  22 us
    dot_general x4, matrix products, transpose_product(): lax.dot_general(design, right_side, (((0,), (0,)), ((), ())), preferred_e...  21.2 us
  transfers between devices with their start and end apart: 6, of which 5 were waited for; matrix products, arithmetic and copies ran while one was open for 2% of the time, Pallas kernels for 0%

profile of v1, /device:TPU:0, one launch (start us, length us, event | category | flops | bytes accessed | tf_op | source)
XLA Modules:
  0.0 918.1 jit_solution(11315641028761405603)
XLA Ops:
  7.2 6.5 fusion.5
  13.8 6.0 fusion.13
  19.8 198.5 %all-gather.7.cloned.1.call-done = f32[28672,128]{1,0:T(8,128)} async-done(((f32[3584,128]{1,0:T(8,128)}), f32[28672,128]{1,0:T(8,128)}) %all-gather.7.cloned.1.call-update) | async-done | bytes 14680080 | tf_op jit(solution)/shard_map/all_gather | solution.py:39
  218.3 7.3 reduce_sum.217
  227.3 5.0 convolution_bitcast_fusion.4
  232.4 4.6 multiply_reduce_fusion
  237.9 6.4 psum.112
  244.4 22.7 %all-reduce.11.cloned.1.call-done = (f32[1024,128]{0,1:T(8,128)}, f32[1024,128]{1,0:T(8,128)}) async-done(((f32[1024,128]{0,1:T(8,128)}, f32[1024,128]{1,0:T(8,128)}), (f32[1024,128]{0,1:T(8,128)}, f32[1024,128]{1,0:T(8,128)})) %all-reduce.11.cloned.1.call-update) | async-done | bytes 1048592 | tf_op jit(solution)/shard_map/psum | solution.py:52
  269.0 22.0 %pmax.28 = f32[]{:T(128)} all-reduce(f32[]{:T(128)} %sqrt_reduce_fusion.3), channel_id=1, replica_groups=mesh['feat'=8,'samp'=4] {'feat'}, use_global_device_ids=true, to_apply=%region_8.0 | all-reduce | flops 1 | bytes 8 | tf_op jit(solution)/shard_map/pmax | solution.py:28
  293.4 6.9 convolution_bitcast_fusion.1
  300.5 198.4 %all-gather.9.cloned.1.call-done = f32[28672,128]{0,1:T(8,128)} async-done(((f32[3584,128]{0,1:T(8,128)}), f32[28672,128]{0,1:T(8,128)}) %all-gather.9.cloned.1.call-update) | async-done | bytes 14680080 | tf_op jit(solution)/shard_map/all_gather | solution.py:39
  498.9 21.7 %copy.19 = f32[16,8,8,3584]{3,2,1,0:T(8,128)} copy(f32[16,8,8,3584]{3,1,2,0:T(8,128)} %bitcast.44) | data formatting | bytes 29360128
  520.6 10.1 %bitcast_reduce_fusion.1 = f32[3584,128]{0,1:T(8,128)} fusion(f32[16,8,8,3584]{3,2,1,0:T(8,128)} %copy.19), kind=kLoop, calls=%fused_computation.1 | loop fusion | flops 3211264 | bytes 16515072 | tf_op jit(solution)/shard_map/reduce_sum | solution.py:39
  530.7 2.7 copy.16
  535.1 5.0 convolution_bitcast_fusion.3
  540.2 31.7 %all-reduce.7.cloned.1.call-done = f32[1024,128]{0,1:T(8,128)} async-done(((f32[1024,128]{0,1:T(8,128)}), f32[1024,128]{0,1:T(8,128)}) %all-reduce.7.cloned.1.call-update) | async-done | bytes 524304 | tf_op jit(solution)/shard_map/psum | solution.py:52
  575.7 6.8 convolution_bitcast_fusion
  586.4 198.1 %all-gather.11.cloned.1.call-done = f32[28672,128]{0,1:T(8,128)} async-done(((f32[3584,128]{0,1:T(8,128)}), f32[28672,128]{0,1:T(8,128)}) %all-gather.11.cloned.1.call-update) | async-done | bytes 14680080 | tf_op jit(solution)/shard_map/all_gather | solution.py:39
  784.5 21.9 %copy.20 = f32[16,8,8,3584]{3,2,1,0:T(8,128)} copy(f32[16,8,8,3584]{3,1,2,0:T(8,128)} %bitcast.43) | data formatting | bytes 29360128
  806.4 9.9 %bitcast_reduce_fusion = f32[3584,128]{0,1:T(8,128)} fusion(f32[16,8,8,3584]{3,2,1,0:T(8,128)} %copy.20), kind=kLoop, calls=%fused_computation | loop fusion | flops 3211264 | bytes 16515072 | tf_op jit(solution)/shard_map/reduce_sum | solution.py:39
  816.3 2.7 copy.17
  821.6 5.1 convolution_bitcast_fusion.2
  832.7 40.0 %all-reduce = (f32[]{:T(128)}, f32[]{:T(128)}, f32[]{:T(128)}, f32[]{:T(128)}, f32[]{:T(128)}, /*index=5*/f32[]{:T(128)}, f32[]{:T(128)}, f32[]{:T(128)}, f32[]{:T(128)}, f32[1]{0:T(128)}, /*index=10*/f32[1]{0:T(128)}) all-reduce(f32[]{:T(128)} %get-tuple-element.20, ...), channel_id=1, replica_groups=mesh['feat'=8,'samp'=4] {'feat','samp'}, use_global_device_ids=true, to_apply=%region_38.0 | all-reduce | flops 11 | bytes 88 | tf_op jit(solution)/shard_map/psum | solution.py:56
  880.1 22.1 %all-reduce.1 = (f32[]{:T(128)}, f32[]{:T(128)}, f32[]{:T(128)}) all-reduce(f32[]{:T(128)} %sqrt_reduce_fusion.4, f32[]{:T(128)} %sqrt_reduce_fusion.5, f32[]{:T(128)} %sqrt_reduce_fusion.6), channel_id=1, replica_groups=mesh['feat'=8,'samp'=4] {'feat'}, use_global_device_ids=true, to_apply=%region_22.0 | all-reduce | flops 3 | bytes 24 | tf_op jit(solution)/shard_map/pmax | solution.py:55
  (56 shorter events, 25.5 us)
Async XLA Ops:
  7.2 6.7 copy-start
  7.2 211.1 %all-gather.7.cloned.1.call-start = ((), (), s32[]{:S(2)}) async-start(), calls=%async_computation.2 | async-start | bytes 16515072 | tf_op jit(solution)/shard_map/all_gather | solution.py:39
  13.8 253.3 %all-reduce.11.cloned.1.call-start = ((), (), s32[]{:S(2)}) async-start(), calls=%async_computation.5 | async-start | bytes 2097152 | tf_op jit(solution)/shard_map/psum | solution.py:52
  232.4 4.7 copy-start.4
  232.4 12.0 %copy-start.6 = (s32[2,1024]{1,0:T(2,128)S(1)}, s32[2,1024]{1,0:T(2,128)}, u32[]{:S(2)}) copy-start(s32[2,1024]{1,0:T(2,128)} %param.8) | copy-start | bytes 24580
  232.4 266.5 %all-gather.9.cloned.1.call-start = ((), (), s32[]{:S(2)}) async-start(), calls=%async_computation.3 | async-start | bytes 16515072 | tf_op jit(solution)/shard_map/all_gather | solution.py:39
  300.3 271.6 %all-reduce.7.cloned.1.call-start = ((), (), s32[]{:S(2)}) async-start(), calls=%async_computation | async-start | bytes 1048576 | tf_op jit(solution)/shard_map/psum | solution.py:52
  540.2 244.4 %all-gather.11.cloned.1.call-start = ((), (), s32[]{:S(2)}) async-start(), calls=%async_computation.4 | async-start | bytes 16515072 | tf_op jit(solution)/shard_map/all_gather | solution.py:39
  574.9 0.8 copy-start.2
  574.9 8.1 copy-start.5
  582.6 295.8 %all-reduce.9.cloned.1.call-start = ((), (), s32[]{:S(2)}) async-start(), calls=%async_computation.1 | async-start | bytes 1048576 | tf_op jit(solution)/shard_map/psum | solution.py:52
  820.7 0.9 copy-start.1
  821.6 5.8 copy-start.3
Sparse Core Ops, SparseCore 0:
  13.9 204.3 all-gather.6
  232.5 34.5 all-reduce.10
  300.4 198.4 all-gather.8
  540.3 31.5 all-reduce.6
  582.7 201.7 all-gather.10
  826.9 31.6 all-reduce.8
